TPU v7x, 128 devices: a whole 4x4x4 slice. The times are simulated.
128 devices in a mesh: dp: 8 (over x, core), tensor: 8 (over y_lo, z), section: 2 (over y_hi).
Axes of the slice: x: 4, y: 4 (y_hi: 2, y_lo: 2; y = y_hi * 2 + y_lo), z: 4, core: 2. Of those that a mesh axis runs over, the one named last changes fastest.
Arguments:
- patches: bfloat16 [32, 256, 1152], P(('dp', 'section'), 'tensor'), may hold values from -6 to 6
- teacher: int32 [32, 7], P(('dp', 'section')), may hold values from 0 to 255
- proj_w: bfloat16 [1152, 4096], P(None, ('dp', 'tensor', 'section')), may hold values from -0.1875 to 0.1875
- norm_gain: bfloat16 [4096], replicated, may hold values from 0.25 to 1.75
- wq: bfloat16 [4096, 4096], P(('dp', 'section'), 'tensor'), may hold values from -0.09375 to 0.09375
- wk: bfloat16 [4096, 4096], P(('dp', 'section'), 'tensor'), may hold values from -0.09375 to 0.09375
- wv: bfloat16 [4096, 4096], P(('dp', 'section'), 'tensor'), may hold values from -0.09375 to 0.09375
- wo: bfloat16 [4096, 4096], P('tensor', ('dp', 'section')), may hold values from -0.09375 to 0.09375
- start_row: bfloat16 [4096], replicated, may hold values from -6 to 6
- action_table: bfloat16 [256, 4096], replicated, may hold values from -6 to 6
- final_gain: bfloat16 [4096], replicated, may hold values from 0.25 to 1.75
- head_w: bfloat16 [4096, 256], replicated, may hold values from -0.25 to 0.25
Outputs:
- hidden_out: bfloat16 [32, 256, 4096], P(('dp', 'section'), 'tensor')
- loss: float32 [32, 7], P(('dp', 'section'))
All inputs are finite; a program needn't handle non-finite values.
Results may differ from a plain program's by a relative error of at most 0.0054.
Values may be sent and summed in bfloat16 or wider, within the bound.
No kernel may reach another device: no remote copies, remote signals or barrier semaphores. Data moves between devices by JAX's collectives and lax.ppermute only.
A program may use at most 128 MiB of HBM per device.

v0:
```python
import math
import jax
import jax.numpy as jnp
from jax import lax
from jax.sharding import PartitionSpec as P

D = 4096
HD = 128
V = 1152
P_SIZE = 256
BINS = 256
ADIM = 7
SLOTS = 8
eps = 1e-05


def joined_along(parts, dim):
    dims = list(parts.shape[1:])
    dims[dim] *= parts.shape[0]
    return jnp.moveaxis(parts, 0, dim).reshape(dims)


def from_everyone(shard, axis):
    devices = lax.axis_size(axis)
    return lax.all_to_all(
        jnp.broadcast_to(shard[None], (devices, *shard.shape)), axis, 0, 0, tiled=True
    )


def gathered_copies(shard, axis, dim):
    return joined_along(from_everyone(shard, axis), dim)


def side_by_side(arrays, axis, dim, along):
    widths = [a.shape[along] for a in arrays]
    both = jnp.concatenate(arrays, axis=along)
    filled = lax.all_gather(both, axis, axis=dim, tiled=True)
    return tuple(jnp.split(filled, [sum(widths[:k]) for k in range(1, len(widths))], axis=along))


def over_copies(shard, axis):
    everything = from_everyone(shard, axis)
    return jnp.sum(everything.astype(jnp.float32), axis=0)


def normalize(rows, gain):
    rows = rows.astype(jnp.float32)
    factor = lax.rsqrt(jnp.mean(rows * rows, axis=-1, keepdims=True) + eps)
    return rows * factor * gain.astype(jnp.float32)


def action_rows(teacher, start_row, action_table):
    frames = teacher.shape[0]
    onehot = (teacher[..., None] == jnp.arange(BINS, dtype=jnp.int32)).astype(jnp.bfloat16)
    looked = jnp.dot(onehot.reshape(-1, BINS), action_table, preferred_element_type=jnp.float32)
    looked = looked.astype(jnp.bfloat16).reshape(frames, ADIM, D)
    start = jnp.broadcast_to(start_row.reshape(1, 1, D), (frames, 1, D))
    return jnp.concatenate([start, looked], axis=1)


def embed(source_rows, proj_w):
    flat = source_rows.reshape(-1, V)
    result = jnp.dot(
        flat,
        lax.all_gather(proj_w, ("dp", "tensor", "section"), axis=1, tiled=True),
        preferred_element_type=jnp.float32,
    )
    return result.astype(jnp.bfloat16).reshape(source_rows.shape[0], source_rows.shape[1], D)


def on_device(
    patches, teacher, proj_w, norm_gain, wq, wk, wv, wo, start_row, action_table, final_gain, head_w
):
    frames = patches.shape[0]
    local_patches = patches.shape[1]
    length = P_SIZE + SLOTS
    all_patches = gathered_copies(patches, "tensor", 1)
    embedded_all = embed(all_patches, proj_w)
    embedded_own = lax.dynamic_slice_in_dim(
        embedded_all, lax.axis_index("tensor") * local_patches, local_patches, 1
    )
    actions = action_rows(teacher, start_row, action_table)
    stream = jnp.concatenate([embedded_all, actions], axis=1)
    normed = normalize(stream, norm_gain).astype(jnp.bfloat16).reshape(-1, D)
    local_width = wq.shape[1]
    full_query, full_key, full_value = side_by_side((wq, wk, wv), ("dp", "section"), 0, 1)
    projected = tuple(
        (
            jnp.dot(normed, weight, preferred_element_type=jnp.float32)
            for weight in (full_query, full_key, full_value)
        )
    )
    heads_local = local_width // HD
    queries, keys_all, values_all = [
        part.astype(jnp.bfloat16).reshape(frames, length, heads_local, HD) for part in projected
    ]
    inv_root = 1.0 / math.sqrt(HD)
    scores = (
        jnp.einsum("fqhd,fkhd->fhqk", queries, keys_all, preferred_element_type=jnp.float32)
        * inv_root
    )
    positions = jnp.arange(length, dtype=jnp.int32)
    causal = positions[:, None] >= positions[None, :]
    scores = jnp.where(causal[None, None], scores, -1e30)
    weights = jax.nn.softmax(scores, axis=-1).astype(jnp.bfloat16)
    mixed = jnp.einsum("fhqk,fkhd->fqhd", weights, values_all, preferred_element_type=jnp.float32)
    mixed = mixed.astype(jnp.bfloat16).reshape(frames, length, local_width)
    wo_rows = lax.all_gather(wo, ("dp", "section"), axis=1, tiled=True)
    patch_major = jnp.transpose(mixed[:, :P_SIZE], (1, 0, 2))
    product = jnp.dot(
        patch_major.reshape(-1, local_width), wo_rows, preferred_element_type=jnp.float32
    )
    own_rows = lax.psum_scatter(
        product.reshape(local_patches * lax.axis_size("tensor"), frames, D),
        "tensor",
        scatter_dimension=0,
        tiled=True,
    )
    patch_update = jnp.transpose(own_rows, (1, 0, 2))
    action_mixed = mixed[:, P_SIZE : P_SIZE + ADIM].reshape(-1, local_width)
    action_part = jnp.dot(action_mixed, wo_rows, preferred_element_type=jnp.float32).reshape(
        frames, ADIM, D
    )
    hidden_out = (embedded_own.astype(jnp.float32) + patch_update).astype(jnp.bfloat16)
    action_update = over_copies(action_part.astype(jnp.bfloat16), "tensor").astype(jnp.float32)
    acted = actions[:, :ADIM].astype(jnp.float32) + action_update
    final = normalize(acted, final_gain).astype(jnp.bfloat16).reshape(-1, D)
    logits = jnp.dot(final, head_w, preferred_element_type=jnp.float32).reshape(frames, ADIM, BINS)
    chosen = (teacher[..., None] == jnp.arange(BINS, dtype=jnp.int32)).astype(jnp.float32)
    picked = jnp.sum(logits * chosen, axis=-1)
    loss = jax.nn.logsumexp(logits, axis=-1) - picked
    return (hidden_out, loss)


def solution(mesh):
    return jax.shard_map(
        on_device,
        mesh=mesh,
        in_specs=(
            P(("dp", "section"), "tensor", None),
            P(("dp", "section"), None),
            P(None, ("dp", "tensor", "section")),
            P(),
            P(("dp", "section"), "tensor"),
            P(("dp", "section"), "tensor"),
            P(("dp", "section"), "tensor"),
            P("tensor", ("dp", "section")),
            P(),
            P(),
            P(),
            P(),
        ),
        out_specs=(P(("dp", "section"), "tensor", None), P(("dp", "section"), None)),
        check_vma=False,
    )
```

profile of v0, /device:TPU:1, one launch (start us, length us, event | category | flops | bytes accessed | tf_op | source)
XLA Modules:
  0.0 596.9 jit_solution(13776952633061691405)
XLA Ops:
  8.0 2.0 pad_maximum_fusion
  10.0 2.0 broadcast_in_dim.14
  12.1 6.9 %all-to-all-start = ((bf16[8,2,32,1152]{3,2,1,0:T(8,128)(2,1)}), bf16[8,2,32,1152]{3,2,1,0:T(8,128)(2,1)S(1)}, u32[]{:S(2)}, u32[]{:S(2)}) async-start(bf16[8,2,32,1152]{3,2,1,0:T(8,128)(2,1)} %broadcast_in_dim.14), calls=%async_computation | async-start | bytes 2359296 | tf_op jit(solution)/shard_map/all_to_all | solution.py:25
  20.3 15.0 %all-to-all-done = bf16[8,2,32,1152]{3,2,1,0:T(8,128)(2,1)S(1)} async-done(((bf16[8,2,32,1152]{3,2,1,0:T(8,128)(2,1)}), bf16[8,2,32,1152]{3,2,1,0:T(8,128)(2,1)S(1)}, u32[]{:S(2)}, u32[]{:S(2)}) %all-to-all-start) | async-done | bytes 1179680 | tf_op jit(solution)/shard_map/all_to_all | solution.py:25
  35.4 295.1 %all-gather.4.cloned.1.call-done = bf16[1152,4096]{0,1:T(8,128)(2,1)} async-done(((bf16[1152,32]{0,1:T(8,128)(2,1)}), bf16[1152,4096]{0,1:T(8,128)(2,1)}) %all-gather.4.cloned.1.call-update) | async-done | bytes 9437200 | tf_op jit(solution)/shard_map/all_gather | solution.py:65
  330.5 9.5 %convolution_convert_fusion = bf16[512,4096]{1,0:T(8,128)(2,1)S(1)} fusion(bf16[512,1152]{1,0:T(8,128)(2,1)S(1)} %bitcast.44, bf16[1152,4096]{0,1:T(8,128)(2,1)} %all-gather.4.cloned.1.call-done), kind=kOutput, calls=%fused_computation.5 | convolution fusion | flops 4833935360 | bytes 14811136 | tf_op jit(solution)/shard_map/dot_general | solution.py:63
  340.1 1.9 copy-done.2
  342.0 1.3 multiply_reduce_fusion
  343.4 2.8 maximum_convert_fusion
  346.2 3.6 fusion.2
  349.8 70.9 %all-gather.6.cloned.1.call-done = bf16[4096,1536]{1,0:T(8,128)(2,1)} async-done(((bf16[256,1536]{1,0:T(8,128)(2,1)}), bf16[4096,1536]{1,0:T(8,128)(2,1)}) %all-gather.6.cloned.1.call-update) | async-done | bytes 12582928 | tf_op jit(solution)/shard_map/all_gather | solution.py:37
  420.6 5.9 fusion.23
  426.7 5.9 fusion.26
  432.8 5.9 fusion.20
  439.5 1.3 fusion.40
  441.8 37.4 %all-gather.8.cloned.1.call-done = bf16[512,4096]{1,0:T(8,128)(2,1)} async-done(((bf16[512,256]{1,0:T(8,128)(2,1)}), bf16[512,4096]{1,0:T(8,128)(2,1)}) %all-gather.8.cloned.1.call-update) | async-done | bytes 4194320 | tf_op jit(solution)/shard_map/all_gather | solution.py:108
  479.2 7.8 %fusion.10 = f32[256,2,4096]{2,0,1:T(8,128)} fusion(bf16[512,4096]{1,0:T(8,128)(2,1)} %all-gather.8.cloned.1.call-done, bf16[2,264,512]{2,1,0:T(8,128)(2,1)S(1)} %bitcast.42), kind=kOutput, calls=%fused_computation.16 | convolution fusion | flops 2147483648 | bytes 13107200 | tf_op jit(solution)/shard_map/dot_general | solution.py:110
  487.0 2.9 convolution_convert_fusion.1
  490.0 1.8 broadcast_in_dim.22
  491.8 4.2 all-to-all-start.1
  496.2 25.0 %all-to-all-done.1 = bf16[8,2,7,4096]{3,1,2,0:T(2,128)(2,1)S(1)} async-done(((bf16[8,2,7,4096]{3,1,2,0:T(2,128)(2,1)}), bf16[8,2,7,4096]{3,1,2,0:T(2,128)(2,1)S(1)}, u32[]{:S(2)}, u32[]{:S(2)}) %all-to-all-start.1) | async-done | bytes 917536 | tf_op jit(solution)/shard_map/all_to_all | solution.py:25
  522.6 2.2 fusion.41
  525.6 62.5 %reduce-scatter.2.cloned.1.call-done = f32[32,2,4096]{2,0,1:T(8,128)} async-done(((f32[256,2,4096]{2,0,1:T(8,128)}), f32[32,2,4096]{2,0,1:T(8,128)}) %reduce-scatter.2.cloned.1.call-update) | async-done | bytes 1048592 | tf_op jit(solution)/shard_map/reduce_scatter | solution.py:113
  588.1 2.2 fusion.30
  (47 shorter events, 6.9 us)
Async XLA Ops:
  7.2 12.6 %copy-start = (bf16[256,4096]{1,0:T(8,128)(2,1)S(1)}, bf16[256,4096]{1,0:T(8,128)(2,1)}, u32[]{:S(2)}) copy-start(bf16[256,4096]{1,0:T(8,128)(2,1)} %param.21) | copy-start | bytes 6291460
  7.2 12.5 %copy-start.6 = (s32[2,7]{1,0:T(2,128)S(1)}, s32[2,7]{1,0:T(2,128)}, u32[]{:S(2)}) copy-start(s32[2,7]{1,0:T(2,128)} %param.13) | copy-start | bytes 172
  7.2 323.3 %all-gather.4.cloned.1.call-start = ((), (), s32[]{:S(2)}) async-start(), calls=%async_computation.3 | async-start | bytes 9510912 | tf_op jit(solution)/shard_map/all_gather | solution.py:65
  7.9 12.3 %copy-start.4 = (bf16[4096]{0:T(1024)(128)(2,1)S(1)}, bf16[4096]{0:T(1024)(128)(2,1)}, u32[]{:S(2)}) copy-start(bf16[4096]{0:T(1024)(128)(2,1)} %param.15) | copy-start | bytes 24580
  7.9 412.7 %all-gather.6.cloned.1.call-start = ((), (), s32[]{:S(2)}) async-start(), calls=%async_computation.4 | async-start | bytes 13369344 | tf_op jit(solution)/shard_map/all_gather | solution.py:37
  12.1 23.2 %all-to-all-start = ((bf16[8,2,32,1152]{3,2,1,0:T(8,128)(2,1)}), bf16[8,2,32,1152]{3,2,1,0:T(8,128)(2,1)S(1)}, u32[]{:S(2)}, u32[]{:S(2)}) async-start(bf16[8,2,32,1152]{3,2,1,0:T(8,128)(2,1)} %broadcast_in_dim.14), calls=%async_computation | async-start | bytes 2359296 | tf_op jit(solution)/shard_map/all_to_all | solution.py:25
  18.9 460.3 %all-gather.8.cloned.1.call-start = ((), (), s32[]{:S(2)}) async-start(), calls=%async_computation.5 | async-start | bytes 4456448 | tf_op jit(solution)/shard_map/all_gather | solution.py:108
  19.7 568.5 %reduce-scatter.2.cloned.1.call-start = ((), (), s32[]{:S(2)}) async-start(), calls=%async_computation.6 | async-start | bytes 9437184 | tf_op jit(solution)/shard_map/reduce_scatter | solution.py:113
  330.5 9.5 %copy-start.3 = (bf16[4096]{0:T(1024)(128)(2,1)S(1)}, bf16[4096]{0:T(1024)(128)(2,1)}, u32[]{:S(2)}) copy-start(bf16[4096]{0:T(1024)(128)(2,1)} %param.20) | copy-start | bytes 24580
  340.0 1.9 copy-start.2
  487.0 9.2 %copy-start.5 = (bf16[4096]{0:T(1024)(128)(2,1)S(1)}, bf16[4096]{0:T(1024)(128)(2,1)}, u32[]{:S(2)}) copy-start(bf16[4096]{0:T(1024)(128)(2,1)} %param.22) | copy-start | bytes 24580
  490.0 100.4 %copy-start.1 = (bf16[256,4096]{1,0:T(8,128)(2,1)S(1)}, bf16[256,4096]{1,0:T(8,128)(2,1)}, u32[]{:S(2)}) copy-start(bf16[256,4096]{1,0:T(8,128)(2,1)} %param.21) | copy-start | bytes 6291460
  491.8 29.3 %all-to-all-start.1 = ((bf16[8,2,7,4096]{3,1,2,0:T(2,128)(2,1)}), bf16[8,2,7,4096]{3,1,2,0:T(2,128)(2,1)S(1)}, u32[]{:S(2)}, u32[]{:S(2)}) async-start(bf16[8,2,7,4096]{3,1,2,0:T(2,128)(2,1)} %broadcast_in_dim.22), calls=%async_computation.2 | async-start | bytes 1835008 | tf_op jit(solution)/shard_map/all_to_all | solution.py:25
Sparse Core Ops, SparseCore 0:
  9.7 320.7 all-gather.3
  332.9 87.6 all-gather.5
  422.9 56.2 all-gather.7
  487.1 100.9 reduce-scatter.1
where the time goes:
time: 597 us
  waiting for transfers between devices  507 us (85%)
  matrix products  42.1 us (7%)
  other arithmetic  15.6 us (3%)
  between operations  14 us (2%)
  starting transfers between devices  11.2 us (2%)
  local copies, waits for them, and re-layouts  6.82 us (1%)
    all_gather x1, waiting for transfers between devices, embed(): lax.all_gather(proj_w, ('dp', 'tensor', 'section'), axis=1, tiled=True)  295 us
    all_gather x1, waiting for transfers between devices, side_by_side(): filled = lax.all_gather(both, axis, axis=dim, tiled=True)  70.9 us
    reduce_scatter x1, waiting for transfers between devices, on_device(): lax.psum_scatter(product.reshape(local_patches * lax.axis_size('tensor'),...  62.5 us
    all_to_all x2, waiting for transfers between devices, from_everyone(): lax.all_to_all(jnp.broadcast_to(shard[None], (devices, *shard.shape)), ax...  39.9 us
    all_gather x1, waiting for transfers between devices, on_device(): wo_rows = lax.all_gather(wo, ('dp', 'section'), axis=1, tiled=True)  37.4 us
    dot_general x3, matrix products, on_device(): jnp.dot(normed, weight, preferred_element_type=jnp.float32)  17.7 us
  transfers between devices with their start and end apart: 6, of which 6 were waited for; matrix products, arithmetic and copies ran while one was open for 9% of the time, Pallas kernels for 0%

commit v1 on v0

--- a/solution.py
+++ b/solution.py
@@ -62,7 +62,15 @@
     flat = source_rows.reshape(-1, V)
     result = jnp.dot(
         flat,
-        lax.all_gather(proj_w, ("dp", "tensor", "section"), axis=1, tiled=True),
+        jnp.concatenate(
+            lax.all_to_all(
+                jnp.stack([proj_w] * lax.axis_size(("dp", "tensor", "section"))),
+                ("dp", "tensor", "section"),
+                0,
+                0,
+            ),
+            axis=1,
+        ),
         preferred_element_type=jnp.float32,
     )
     return result.astype(jnp.bfloat16).reshape(source_rows.shape[0], source_rows.shape[1], D)

time: 597 us -> 396 us (0.66)
  waiting for transfers between devices: 507 us -> 270 us
  blocking collectives: 0 us -> 26.3 us
    all_gather x1 -> x0, waiting for transfers between devices: 295 us -> none  [embed(): lax.all_gather(proj_w, ('dp', 'tensor', 'section'), axis=1, tiled=True)]
    all_to_all x0 -> x1, waiting for transfers between devices: none -> 138 us  [embed(): lax.all_to_all(jnp.stack([proj_w] * lax.axis_size(('dp', 'tensor', 'secti...]
    all_gather x1, waiting for transfers between devices: 70.9 us -> 2.31 us  [side_by_side(): filled = lax.all_gather(both, axis, axis=dim, tiled=True)]
    all_to_all x0 -> x1, blocking collectives: none -> 26.3 us  [from_everyone(): lax.all_to_all(jnp.broadcast_to(shard[None], (devices, *shard.shape)), ax...]
    all_to_all x2 -> x1, waiting for transfers between devices: 39.9 us -> 25 us  [from_everyone(): lax.all_to_all(jnp.broadcast_to(shard[None], (devices, *shard.shape)), ax...]
    all_to_all x0 -> x1, starting transfers between devices: none -> 12.5 us  [embed(): lax.all_to_all(jnp.stack([proj_w] * lax.axis_size(('dp', 'tensor', 'secti...]
    all_to_all x2 -> x1, starting transfers between devices: 11 us -> 4.17 us  [from_everyone(): lax.all_to_all(jnp.broadcast_to(shard[None], (devices, *shard.shape)), ax...]
  transfers between devices with their start and end apart: 6 -> 5, of which waited for: 6 -> 5; matrix products, arithmetic and copies ran while one was open for 9% -> 14% of each run, Pallas kernels for 0% -> 0%
where the time goes in v1:
time: 396 us
  waiting for transfers between devices  270 us (68%)
  matrix products  42.2 us (11%)
  blocking collectives  26.3 us (7%)
  starting transfers between devices  16.8 us (4%)
  other arithmetic  15.9 us (4%)
  between operations  14 us (4%)
  local copies, waits for them, and re-layouts  10.2 us (3%)
    all_to_all x1, waiting for transfers between devices, embed(): lax.all_to_all(jnp.stack([proj_w] * lax.axis_size(('dp', 'tensor', 'secti...  138 us
    reduce_scatter x1, waiting for transfers between devices, on_device(): lax.psum_scatter(product.reshape(local_patches * lax.axis_size('tensor'),...  62.5 us
    all_gather x1, waiting for transfers between devices, on_device(): wo_rows = lax.all_gather(wo, ('dp', 'section'), axis=1, tiled=True)  42.2 us
    all_to_all x1, blocking collectives, from_everyone(): lax.all_to_all(jnp.broadcast_to(shard[None], (devices, *shard.shape)), ax...  26.3 us
    all_to_all x1, waiting for transfers between devices, from_everyone(): lax.all_to_all(jnp.broadcast_to(shard[None], (devices, *shard.shape)), ax...  25 us
    dot_general x3, matrix products, on_device(): jnp.dot(normed, weight, preferred_element_type=jnp.float32)  17.9 us
    all_to_all x1, starting transfers between devices, embed(): lax.all_to_all(jnp.stack([proj_w] * lax.axis_size(('dp', 'tensor', 'secti...  12.5 us
    dot_general x1, matrix products, embed(): jnp.dot(flat, jnp.concatenate(lax.all_to_all(jnp.stack([proj_w] * lax.axi...  9.53 us
  transfers between devices with their start and end apart: 5, of which 5 were waited for; matrix products, arithmetic and copies ran while one was open for 14% of the time, Pallas kernels for 0%

profile of v1, /device:TPU:1, one launch (start us, length us, event | category | flops | bytes accessed | tf_op | source)
XLA Modules:
  0.0 395.8 jit_solution(8170413930369280385)
XLA Ops:
  7.2 2.2 pad_maximum_fusion
  10.5 26.3 %all_to_all.15 = bf16[8,2,32,1152]{3,2,1,0:T(8,128)(2,1)S(1)} all-to-all(bf16[8,2,32,1152]{3,2,1,0:T(8,128)(2,1)S(1)} %broadcast_in_dim.14), channel_id=1, replica_groups=mesh['dp'=8,'tensor'=8,'section'=2] {'tensor'}, dimensions={0} | all-to-all | bytes 2359296 | tf_op jit(solution)/shard_map/all_to_all | solution.py:25
  36.8 4.3 %stack.2 = bf16[128,1152,32]{1,2,0:T(8,128)(2,1)} broadcast(bf16[1152,32]{0,1:T(8,128)(2,1)S(1)} %copy-done.3), dimensions={1,2} | broadcast | bytes 9510912 | tf_op jit(solution)/shard_map/stack | solution.py:67
  41.1 12.5 %all-to-all-start.1 = ((bf16[128,1152,32]{1,2,0:T(8,128)(2,1)}), bf16[128,1152,32]{1,2,0:T(8,128)(2,1)}, u32[]{:S(2)}, u32[]{:S(2)}) async-start(bf16[128,1152,32]{1,2,0:T(8,128)(2,1)} %stack.2), calls=%async_computation.1 | async-start | bytes 18874368 | tf_op jit(solution)/shard_map/all_to_all | solution.py:66
  55.1 137.8 %all-to-all-done.1 = bf16[128,1152,32]{1,2,0:T(8,128)(2,1)} async-done(((bf16[128,1152,32]{1,2,0:T(8,128)(2,1)}), bf16[128,1152,32]{1,2,0:T(8,128)(2,1)}, u32[]{:S(2)}, u32[]{:S(2)}) %all-to-all-start.1) | async-done | bytes 9437216 | tf_op jit(solution)/shard_map/all_to_all | solution.py:66
  192.8 9.5 %convolution_convert_fusion = bf16[512,4096]{1,0:T(8,128)(2,1)S(1)} fusion(bf16[512,1152]{1,0:T(8,128)(2,1)S(1)} %bitcast.47, bf16[1152,4096]{0,1:T(8,128)(2,1)} %bitcast.3), kind=kOutput, calls=%fused_computation.5 | convolution fusion | flops 4833935360 | bytes 14811136 | tf_op jit(solution)/shard_map/dot_general | solution.py:63
  202.4 1.9 copy-done.2
  204.3 1.3 multiply_reduce_fusion
  205.7 2.9 maximum_convert_fusion
  208.7 3.6 fusion.2
  212.3 2.3 all-gather.3.cloned.1.call-done
  214.6 5.9 %fusion.23 = bf16[528,512]{1,0:T(8,128)(2,1)S(1)} fusion(bf16[528,4096]{1,0:T(8,128)(2,1)} %fusion.2, bf16[4096,1536]{1,0:T(8,128)(2,1)} %all-gather.3.cloned.1.call-done), kind=kOutput, calls=%fused_computation.31 | convolution fusion | flops 2214862848 | bytes 9060352 | tf_op jit(solution)/shard_map/dot_general | solution.py:97
  220.6 5.9 %fusion.26 = bf16[528,512]{1,0:T(8,128)(2,1)S(1)} fusion(bf16[528,4096]{1,0:T(8,128)(2,1)} %fusion.2, bf16[4096,1536]{1,0:T(8,128)(2,1)} %all-gather.3.cloned.1.call-done), kind=kOutput, calls=%fused_computation.32 | convolution fusion | flops 2214862848 | bytes 9060352 | tf_op jit(solution)/shard_map/dot_general | solution.py:97
  226.7 6.1 %fusion.20 = bf16[528,512]{1,0:T(8,128)(2,1)S(1)} fusion(bf16[528,4096]{1,0:T(8,128)(2,1)} %fusion.2, bf16[4096,1536]{1,0:T(8,128)(2,1)} %all-gather.3.cloned.1.call-done), kind=kOutput, calls=%fused_computation.30 | convolution fusion | flops 2214862848 | bytes 9060352 | tf_op jit(solution)/shard_map/dot_general | solution.py:97
  233.6 1.3 fusion.40
  235.9 42.2 %all-gather.5.cloned.1.call-done = bf16[512,4096]{1,0:T(8,128)(2,1)} async-done(((bf16[512,256]{1,0:T(8,128)(2,1)}), bf16[512,4096]{1,0:T(8,128)(2,1)}) %all-gather.5.cloned.1.call-update) | async-done | bytes 4194320 | tf_op jit(solution)/shard_map/all_gather | solution.py:116
  278.1 7.8 %fusion.10 = f32[256,2,4096]{2,0,1:T(8,128)} fusion(bf16[512,4096]{1,0:T(8,128)(2,1)} %all-gather.5.cloned.1.call-done, bf16[2,264,512]{2,1,0:T(8,128)(2,1)S(1)} %bitcast.45), kind=kOutput, calls=%fused_computation.16 | convolution fusion | flops 2147483648 | bytes 13107200 | tf_op jit(solution)/shard_map/dot_general | solution.py:118
  285.9 2.9 convolution_convert_fusion.1
  288.9 1.8 broadcast_in_dim.22
  290.8 4.2 %all-to-all-start.2 = ((bf16[8,2,7,4096]{3,1,2,0:T(2,128)(2,1)}), bf16[8,2,7,4096]{3,1,2,0:T(2,128)(2,1)S(1)}, u32[]{:S(2)}, u32[]{:S(2)}) async-start(bf16[8,2,7,4096]{3,1,2,0:T(2,128)(2,1)} %broadcast_in_dim.22), calls=%async_computation.3 | async-start | bytes 1835008 | tf_op jit(solution)/shard_map/all_to_all | solution.py:25
  295.1 25.0 %all-to-all-done.2 = bf16[8,2,7,4096]{3,1,2,0:T(2,128)(2,1)S(1)} async-done(((bf16[8,2,7,4096]{3,1,2,0:T(2,128)(2,1)}), bf16[8,2,7,4096]{3,1,2,0:T(2,128)(2,1)S(1)}, u32[]{:S(2)}, u32[]{:S(2)}) %all-to-all-start.2) | async-done | bytes 917536 | tf_op jit(solution)/shard_map/all_to_all | solution.py:25
  321.5 2.2 fusion.41
  324.5 62.5 %reduce-scatter.2.cloned.1.call-done = f32[32,2,4096]{2,0,1:T(8,128)} async-done(((f32[256,2,4096]{2,0,1:T(8,128)}), f32[32,2,4096]{2,0,1:T(8,128)}) %reduce-scatter.2.cloned.1.call-update) | async-done | bytes 1048592 | tf_op jit(solution)/shard_map/reduce_scatter | solution.py:121
  387.0 2.2 fusion.30
  (48 shorter events, 7.2 us)
Async XLA Ops:
  7.2 47.3 %copy-start = (bf16[256,4096]{1,0:T(8,128)(2,1)S(1)}, bf16[256,4096]{1,0:T(8,128)(2,1)}, u32[]{:S(2)}) copy-start(bf16[256,4096]{1,0:T(8,128)(2,1)} %param.21) | copy-start | bytes 6291460
  7.2 29.6 %copy-start.3 = (bf16[1152,32]{0,1:T(8,128)(2,1)S(1)}, bf16[1152,32]{0,1:T(8,128)(2,1)}, u32[]{:S(2)}) copy-start(bf16[1152,32]{0,1:T(8,128)(2,1)} %param.14) | copy-start | bytes 221188
  7.2 207.4 %all-gather.3.cloned.1.call-start = ((), (), s32[]{:S(2)}) async-start(), calls=%async_computation.4 | async-start | bytes 13369344 | tf_op jit(solution)/shard_map/all_gather | solution.py:37
  41.1 13.3 %copy-start.7 = (s32[2,7]{1,0:T(2,128)S(1)}, s32[2,7]{1,0:T(2,128)}, u32[]{:S(2)}) copy-start(s32[2,7]{1,0:T(2,128)} %param.13) | copy-start | bytes 172
  41.1 13.8 %copy-start.5 = (bf16[4096]{0:T(1024)(128)(2,1)S(1)}, bf16[4096]{0:T(1024)(128)(2,1)}, u32[]{:S(2)}) copy-start(bf16[4096]{0:T(1024)(128)(2,1)} %param.15) | copy-start | bytes 24580
  41.1 151.8 %all-to-all-start.1 = ((bf16[128,1152,32]{1,2,0:T(8,128)(2,1)}), bf16[128,1152,32]{1,2,0:T(8,128)(2,1)}, u32[]{:S(2)}, u32[]{:S(2)}) async-start(bf16[128,1152,32]{1,2,0:T(8,128)(2,1)} %stack.2), calls=%async_computation.1 | async-start | bytes 18874368 | tf_op jit(solution)/shard_map/all_to_all | solution.py:66
  53.6 224.6 %all-gather.5.cloned.1.call-start = ((), (), s32[]{:S(2)}) async-start(), calls=%async_computation.5 | async-start | bytes 4456448 | tf_op jit(solution)/shard_map/all_gather | solution.py:116
  54.3 332.7 %reduce-scatter.2.cloned.1.call-start = ((), (), s32[]{:S(2)}) async-start(), calls=%async_computation.6 | async-start | bytes 9437184 | tf_op jit(solution)/shard_map/reduce_scatter | solution.py:121
  192.8 9.6 %copy-start.4 = (bf16[4096]{0:T(1024)(128)(2,1)S(1)}, bf16[4096]{0:T(1024)(128)(2,1)}, u32[]{:S(2)}) copy-start(bf16[4096]{0:T(1024)(128)(2,1)} %param.20) | copy-start | bytes 24580
  202.4 1.9 copy-start.2
  285.9 9.2 %copy-start.6 = (bf16[4096]{0:T(1024)(128)(2,1)S(1)}, bf16[4096]{0:T(1024)(128)(2,1)}, u32[]{:S(2)}) copy-start(bf16[4096]{0:T(1024)(128)(2,1)} %param.22) | copy-start | bytes 24580
  288.9 100.4 %copy-start.1 = (bf16[256,4096]{1,0:T(8,128)(2,1)S(1)}, bf16[256,4096]{1,0:T(8,128)(2,1)}, u32[]{:S(2)}) copy-start(bf16[256,4096]{1,0:T(8,128)(2,1)} %param.21) | copy-start | bytes 6291460
  290.8 29.3 %all-to-all-start.2 = ((bf16[8,2,7,4096]{3,1,2,0:T(2,128)(2,1)}), bf16[8,2,7,4096]{3,1,2,0:T(2,128)(2,1)S(1)}, u32[]{:S(2)}, u32[]{:S(2)}) async-start(bf16[8,2,7,4096]{3,1,2,0:T(2,128)(2,1)} %broadcast_in_dim.22), calls=%async_computation.3 | async-start | bytes 1835008 | tf_op jit(solution)/shard_map/all_to_all | solution.py:25
Sparse Core Ops, SparseCore 0:
  10.4 204.1 all-gather.2
  216.9 61.2 all-gather.4
  286.0 100.9 reduce-scatter.1
